TPU v7x, 32 devices: a whole 2x2x4 slice. The times are simulated.
32 devices in a mesh: group: 1, ctx: 32 (over z, y, x, core).
Axes of the slice: x: 2, y: 2, z: 4, core: 2. Of those that a mesh axis runs over, the one named last changes fastest.
Arguments:
- queries: bfloat16 [2, 64, 128], P('group'), may hold values from -80 to 80
- key_cache: bfloat16 [2, 4096, 512], P('group', 'ctx'), may hold values from -4 to 4
- value_cache: bfloat16 [2, 4096, 512], P('group', 'ctx'), may hold values from -6 to 6
- out_weight: bfloat16 [8192, 4096], P('ctx'), may hold values from -0.125 to 0.125
- hidden_in: bfloat16 [2, 4096], P('group'), may hold values from -45 to 45
- norm_gain: float32 [4096], replicated, may hold values from 0.25 to 1.75
- gate_weight: bfloat16 [32, 4096, 192], P('ctx'), may hold values from -0.09375 to 0.09375
- up_weight: bfloat16 [32, 4096, 192], P('ctx'), may hold values from -0.09375 to 0.09375
- down_weight: bfloat16 [32, 192, 4096], P('ctx'), may hold values from -0.15625 to 0.15625
- routes: int32 [2, 4], P('group'), may hold values from 0 to 3, all different within a row; in each aligned block of 2 rows (0 to 1, 2 to 3, ...) at most 2 rows name the same one
- route_weight: float32 [2, 4], P('group'), may hold values from 0.1 to 1
Outputs:
- mixed: float32 [2, 4096], P('group', 'ctx')
Inputs may be any that keep to these rules, and one draw needn't show every extreme that they name: `routes`: each row names 4 different experts; no expert is named by more than 2 rows, a bound that some block reaches.
All inputs are finite; a program needn't handle non-finite values.
Results may differ from a plain program's by a relative error of at most 0.0035.
Values may be sent and summed in bfloat16 or wider, within the bound.
No kernel may reach another device: no remote copies, remote signals or barrier semaphores. Data moves between devices by JAX's collectives and lax.ppermute only.
A program may use at most 64 MiB of HBM per device.

v0:
```python
import jax
import jax.numpy as jnp
from jax import lax
from jax.sharding import PartitionSpec as P

QUARTERS = 8
eps = 1e-06


def slot_numbers(routes, expert_count):
    flat_routes = routes.reshape(-1)
    onehot = (flat_routes[:, None] == jnp.arange(expert_count, dtype=jnp.int32)[None, :]).astype(
        jnp.int32
    )
    before = jnp.cumsum(onehot, axis=0) - onehot
    return jnp.sum(before * onehot, axis=1)


def body(
    queries,
    key_cache,
    value_cache,
    out_weight,
    hidden_in,
    norm_gain,
    gate_weight,
    up_weight,
    down_weight,
    routes,
    route_weight,
):
    devices = lax.axis_size("ctx")
    my_index = lax.axis_index("ctx")
    seq_count, head_count, head_dim = queries.shape
    kv_heads = key_cache.shape[2] // head_dim
    group_size = head_count // kv_heads
    model_width = hidden_in.shape[1]
    local_len = key_cache.shape[1]
    query_view = queries.reshape(seq_count, kv_heads, group_size, head_dim)
    key_view = key_cache.reshape(seq_count, local_len, kv_heads, head_dim)
    value_view = value_cache.reshape(seq_count, local_len, kv_heads, head_dim)
    scores = jnp.einsum(
        "sgjd,scgd->sgjc", query_view, key_view, preferred_element_type=jnp.float32
    ) * head_dim ** (-0.5)
    row_peak = lax.pmax(jnp.max(scores, axis=-1), "ctx")
    numer = jnp.exp(scores - row_peak[..., None])
    denom_part = jnp.sum(numer, axis=-1)
    partial_value = jnp.einsum(
        "sgjc,scgd->sgjd",
        numer.astype(jnp.bfloat16),
        value_view,
        preferred_element_type=jnp.float32,
    )
    partial_value = partial_value.reshape(seq_count, head_count * head_dim)
    feat_dev = head_count * head_dim // devices
    feat_start = my_index * feat_dev
    summed, denoms = lax.psum((partial_value, denom_part), "ctx")
    attn_mine = lax.dynamic_slice_in_dim(summed, feat_start, feat_dev, 1)
    spread_denoms = jnp.repeat(denoms.reshape(seq_count, head_count), head_dim, axis=1)
    mine_denoms = lax.dynamic_slice_in_dim(spread_denoms, feat_start, feat_dev, 1)
    attended = (attn_mine / mine_denoms).astype(jnp.bfloat16)
    proj_part = jnp.dot(attended, out_weight, preferred_element_type=jnp.float32)
    col_dev = model_width // devices
    col_start = my_index * col_dev
    projected = lax.psum(proj_part, "ctx")
    resid = hidden_in.astype(jnp.float32) + projected
    inverse_rms = lax.rsqrt(jnp.mean(resid * resid, axis=-1, keepdims=True) + eps)
    normed = (resid * inverse_rms * norm_gain).astype(jnp.bfloat16)
    resid_mine = lax.dynamic_slice_in_dim(resid, col_start, col_dev, 1)
    expert_count = devices // QUARTERS
    top_count = routes.shape[1]
    capacity = min(2 * seq_count * top_count // expert_count, seq_count)
    expert = my_index // QUARTERS
    slot_index = slot_numbers(routes, expert_count)
    flat_routes = routes.reshape(-1)
    token_of = jnp.arange(seq_count * top_count, dtype=jnp.int32) // top_count
    matches = (
        (flat_routes[None, :] == expert)
        & (slot_index[None, :] == jnp.arange(capacity, dtype=jnp.int32)[:, None])
    ).astype(jnp.float32)
    owners = (token_of[:, None] == jnp.arange(seq_count, dtype=jnp.int32)[None, :]).astype(
        jnp.float32
    )
    select = jnp.dot(matches, owners, precision=lax.Precision.HIGHEST)
    slot_weight = jnp.dot(matches, route_weight.reshape(-1), precision=lax.Precision.HIGHEST)
    picked_rows = jnp.dot(
        select.astype(jnp.bfloat16), normed, preferred_element_type=jnp.float32
    ).astype(jnp.bfloat16)
    gate_act = jnp.dot(picked_rows, gate_weight[0], preferred_element_type=jnp.float32)
    up_act = jnp.dot(picked_rows, up_weight[0], preferred_element_type=jnp.float32)
    hidden = (jax.nn.silu(gate_act) * up_act).astype(jnp.bfloat16)
    expert_out = (
        jnp.dot(hidden, down_weight[0], preferred_element_type=jnp.float32) * slot_weight[:, None]
    )
    received = lax.all_to_all(
        expert_out.astype(jnp.bfloat16), "ctx", split_axis=1, concat_axis=0, tiled=True
    ).astype(expert_out.dtype)
    quarter_ids = jnp.arange(QUARTERS, dtype=jnp.int32)[None, None, :]
    shard_rows = (routes[:, :, None] * QUARTERS + quarter_ids) * capacity + slot_index.reshape(
        seq_count, top_count
    )[:, :, None]
    moe_mine = jnp.sum(received[shard_rows], axis=(1, 2))
    return resid_mine + moe_mine


def solution(mesh):
    in_specs = (
        P("group", None, None),
        P("group", "ctx", None),
        P("group", "ctx", None),
        P("ctx", None),
        P("group", None),
        P(),
        P("ctx", None, None),
        P("ctx", None, None),
        P("ctx", None, None),
        P("group", None),
        P("group", None),
    )
    out_specs = P("group", "ctx")
    return jax.shard_map(body, mesh=mesh, in_specs=in_specs, out_specs=out_specs, check_vma=False)
```

profile of v0, /device:TPU:0, one launch (start us, length us, event | category | flops | bytes accessed | tf_op | source)
XLA Modules:
  0.0 239.1 jit_solution(7500703949883063939)
XLA Ops:
  6.5 0.0 copy-start
  6.5 0.0 all-reduce.2.cloned.1.call-start
  6.5 1.4 fusion.41
  8.0 42.0 %pmax.7 = f32[2,4,16]{2,1,0:T(4,128)S(1)} all-reduce(f32[2,4,16]{2,1,0:T(4,128)S(1)} %get-tuple-element.7), channel_id=1, replica_groups=mesh['group'=1,'ctx'=32] {'ctx'}, use_global_device_ids=true, to_apply=%region_1.0 | all-reduce | flops 128 | bytes 1024 | tf_op jit(solution)/shard_map/pmax | solution.py:45
  50.0 0.0 copy-start.1
  50.0 0.0 copy-start.2
  50.0 1.2 fusion.17
  51.2 0.7 copy.38
  51.9 0.0 all-reduce.2.cloned.1.call-update
  51.9 0.8 broadcast_in_dim_reshape.2
  52.7 0.7 broadcast_multiply_fusion
  53.3 0.2 fusion.22
  53.6 0.8 reshape.100
  54.3 0.2 reduce_window_sum.11
  54.5 0.1 add.95
  54.6 0.1 reshape.87
  54.7 40.0 %psum.22 = f32[2,64]{1,0:T(2,128)S(1)} all-reduce(f32[2,64]{1,0:T(2,128)S(1)} %reshape.87), channel_id=1, replica_groups=mesh['group'=1,'ctx'=32] {'ctx'}, use_global_device_ids=true, to_apply=%region_4.0 | all-reduce | flops 128 | bytes 1024 | tf_op jit(solution)/shard_map/psum | solution.py:57
  94.7 0.1 broadcast_bitcast_fusion
  94.8 0.2 convolution_convert_fusion.1
  95.0 0.1 compare_select_fusion
  95.1 0.1 convolution_bitcast_fusion
  95.2 0.1 reshape.93
  95.3 0.1 copy.37
  95.3 76.0 %all-reduce.2.cloned.1.call-done = f32[2,8192]{1,0:T(2,128)} async-done(((f32[2,8192]{1,0:T(2,128)}), f32[2,8192]{1,0:T(2,128)}) %all-reduce.2.cloned.1.call-update) | async-done | bytes 65552 | tf_op jit(solution)/shard_map/psum | solution.py:57
  171.4 0.0 copy-done
  171.4 1.1 fusion.32
  172.4 41.0 %psum.23 = f32[2,4096]{1,0:T(2,128)S(1)} all-reduce(f32[2,4096]{1,0:T(2,128)S(1)} %fusion.32), channel_id=1, replica_groups=mesh['group'=1,'ctx'=32] {'ctx'}, use_global_device_ids=true, to_apply=%region_5.0 | all-reduce | flops 8192 | bytes 65536 | tf_op jit(solution)/shard_map/psum | solution.py:65
  213.4 0.0 copy-done.1
  213.5 0.1 multiply_reduce_fusion
  213.6 0.0 copy-done.2
  213.6 0.2 convolution_convert_fusion
  213.8 1.9 fusion.4
  215.8 3.7 %fusion.6 = bf16[2,32,128]{2,0,1:T(2,128)(2,1)} fusion(bf16[1,192,4096]{2,1,0:T(8,128)(2,1)} %param.19, bf16[2,4096]{1,0:T(2,128)(2,1)S(1)} %convolution_convert_fusion, bf16[1,4096,192]{1,2,0:T(8,128)(2,1)} %param.18, f32[2]{0:T(128)S(1)} %convolution_bitcast_fusion, f32[2,192]{1,0:T(2,128)S(1)} %fusion.4), kind=kOutput, calls=%fused_computation.10 | convolution fusion | flops 6310144 | bytes 3180040 | tf_op jit(solution)/shard_map/dot_general | solution.py:93
  219.5 4.4 %all-to-all-start = ((bf16[2,32,128]{2,0,1:T(2,128)(2,1)}), bf16[2,32,128]{2,0,1:T(2,128)(2,1)S(1)}, u32[]{:S(2)}, u32[]{:S(2)}) async-start(bf16[2,32,128]{2,0,1:T(2,128)(2,1)} %fusion.6), calls=%async_computation | async-start | bytes 32768 | tf_op jit(solution)/shard_map/all_to_all | solution.py:95
  223.9 7.2 %all-to-all-done = bf16[2,32,128]{2,0,1:T(2,128)(2,1)S(1)} async-done(((bf16[2,32,128]{2,0,1:T(2,128)(2,1)}), bf16[2,32,128]{2,0,1:T(2,128)(2,1)S(1)}, u32[]{:S(2)}, u32[]{:S(2)}) %all-to-all-start) | async-done | bytes 16416 | tf_op jit(solution)/shard_map/all_to_all | solution.py:95
  231.1 0.6 gather_fusion
  231.7 0.6 dynamic-slice_add_fusion
  (8 shorter events, 0.1 us)
Async XLA Ops:
  6.5 164.8 %copy-start = (bf16[256,4096]{1,0:T(8,128)(2,1)S(1)}, bf16[256,4096]{1,0:T(8,128)(2,1)}, u32[]{:S(2)}) copy-start(bf16[256,4096]{1,0:T(8,128)(2,1)} %param.14) | copy-start | bytes 6291460
  6.5 164.8 %all-reduce.2.cloned.1.call-start = ((), (), s32[]{:S(2)}) async-start(), calls=%async_computation.1 | async-start | bytes 131072 | tf_op jit(solution)/shard_map/psum | solution.py:57
  50.0 163.5 %copy-start.1 = (bf16[2,4096]{1,0:T(2,128)(2,1)S(1)}, bf16[2,4096]{1,0:T(2,128)(2,1)}, u32[]{:S(2)}) copy-start(bf16[2,4096]{1,0:T(2,128)(2,1)} %param.15) | copy-start | bytes 49156
  50.0 163.6 %copy-start.2 = (f32[4096]{0:T(1024)S(1)}, f32[4096]{0:T(1024)}, u32[]{:S(2)}) copy-start(f32[4096]{0:T(1024)} %param.16) | copy-start | bytes 49156
  219.5 11.6 %all-to-all-start = ((bf16[2,32,128]{2,0,1:T(2,128)(2,1)}), bf16[2,32,128]{2,0,1:T(2,128)(2,1)S(1)}, u32[]{:S(2)}, u32[]{:S(2)}) async-start(bf16[2,32,128]{2,0,1:T(2,128)(2,1)} %fusion.6), calls=%async_computation | async-start | bytes 32768 | tf_op jit(solution)/shard_map/all_to_all | solution.py:95
Sparse Core Ops, SparseCore 0:
  52.0 119.3 all-reduce.1
where the time goes:
time: 240 us; the launch traced here: 239 us
  blocking collectives  123 us (51%)
  waiting for transfers between devices  83.2 us (35%)
  between operations  13.5 us (6%)
  matrix products  9.84 us (4%)
  starting transfers between devices  4.4 us (2%)
  local copies, waits for them, and re-layouts  3.2 us (1%)
    psum x1, waiting for transfers between devices, body(): summed, denoms = lax.psum((partial_value, denom_part), 'ctx')  76 us
    pmax x1, blocking collectives, body(): row_peak = lax.pmax(jnp.max(scores, axis=-1), 'ctx')  42 us
    psum x1, blocking collectives, body(): projected = lax.psum(proj_part, 'ctx')  41 us
    psum x1, blocking collectives, body(): summed, denoms = lax.psum((partial_value, denom_part), 'ctx')  40 us
    all_to_all x1, waiting for transfers between devices, body(): lax.all_to_all(expert_out.astype(jnp.bfloat16), 'ctx', split_axis=1, conc...  7.16 us
  transfers between devices with their start and end apart: 2, of which 2 were waited for; matrix products, arithmetic and copies ran while one was open for 1% of the time, Pallas kernels for 0%

commit v1 on v0

--- a/solution.py
+++ b/solution.py
@@ -62,7 +62,11 @@
     proj_part = jnp.dot(attended, out_weight, preferred_element_type=jnp.float32)
     col_dev = model_width // devices
     col_start = my_index * col_dev
-    projected = lax.psum(proj_part, "ctx")
+    projected = proj_part
+    for hop in (1, 2, 4, 8, 16):
+        projected = projected + lax.ppermute(
+            projected, "ctx", [(dev, dev ^ hop) for dev in range(32)]
+        )
     resid = hidden_in.astype(jnp.float32) + projected
     inverse_rms = lax.rsqrt(jnp.mean(resid * resid, axis=-1, keepdims=True) + eps)
     normed = (resid * inverse_rms * norm_gain).astype(jnp.bfloat16)

time: 240 us -> 218 us (0.908)
  blocking collectives: 123 us -> 82 us
  waiting for transfers between devices: 83.2 us -> 95.1 us
  starting transfers between devices: 4.4 us -> 12.7 us
    psum x1 -> x0, blocking collectives: 41 us -> none  [body(): projected = lax.psum(proj_part, 'ctx')]
    ppermute x0 -> x5, waiting for transfers between devices: none -> 10.6 us  [body(): lax.ppermute(projected, 'ctx', [(dev, dev ^ hop) for dev in range(32)])]
    ppermute x0 -> x5, starting transfers between devices: none -> 8.26 us  [body(): lax.ppermute(projected, 'ctx', [(dev, dev ^ hop) for dev in range(32)])]
  transfers between devices with their start and end apart: 2 -> 7, of which waited for: 2 -> 7; matrix products, arithmetic and copies ran while one was open for 1% -> 1% of each run, Pallas kernels for 0% -> 0%
where the time goes in v1:
time: 218 us
  waiting for transfers between devices  95.1 us (44%)
  blocking collectives  82 us (38%)
  between operations  13.5 us (6%)
  starting transfers between devices  12.7 us (6%)
  matrix products  9.81 us (4%)
  local copies, waits for them, and re-layouts  2.51 us (1%)
    psum x1, waiting for transfers between devices, body(): summed, denoms = lax.psum((partial_value, denom_part), 'ctx')  77.3 us
    pmax x1, blocking collectives, body(): row_peak = lax.pmax(jnp.max(scores, axis=-1), 'ctx')  42 us
    psum x1, blocking collectives, body(): summed, denoms = lax.psum((partial_value, denom_part), 'ctx')  39.9 us
    ppermute x5, waiting for transfers between devices, body(): lax.ppermute(projected, 'ctx', [(dev, dev ^ hop) for dev in range(32)])  10.6 us
    ppermute x5, starting transfers between devices, body(): lax.ppermute(projected, 'ctx', [(dev, dev ^ hop) for dev in range(32)])  8.26 us
    all_to_all x1, waiting for transfers between devices, body(): lax.all_to_all(expert_out.astype(jnp.bfloat16), 'ctx', split_axis=1, conc...  7.16 us
    all_to_all x1, starting transfers between devices, body(): lax.all_to_all(expert_out.astype(jnp.bfloat16), 'ctx', split_axis=1, conc...  4.47 us
  transfers between devices with their start and end apart: 7, of which 7 were waited for; matrix products, arithmetic and copies ran while one was open for 1% of the time, Pallas kernels for 0%

profile of v1, /device:TPU:0, one launch (start us, length us, event | category | flops | bytes accessed | tf_op | source)
XLA Modules:
  0.0 217.5 jit_solution(10226316898114296161)
XLA Ops:
  6.5 0.0 copy-start
  6.5 0.0 all-reduce.2.cloned.1.call-start
  6.5 1.4 fusion.41
  8.0 42.0 %pmax.7 = f32[2,4,16]{2,1,0:T(4,128)S(1)} all-reduce(f32[2,4,16]{2,1,0:T(4,128)S(1)} %get-tuple-element.7), channel_id=1, replica_groups=mesh['group'=1,'ctx'=32] {'ctx'}, use_global_device_ids=true, to_apply=%region_1.0 | all-reduce | flops 128 | bytes 1024 | tf_op jit(solution)/shard_map/pmax | solution.py:45
  50.0 1.2 fusion.17
  51.2 0.0 copy-start.3
  51.2 0.0 copy-start.1
  51.2 0.7 copy.38
  51.8 0.0 copy-start.2
  51.8 0.0 all-reduce.2.cloned.1.call-update
  51.9 0.2 fusion.22
  52.0 0.8 broadcast_in_dim_reshape.2
  52.8 0.7 broadcast_multiply_fusion
  53.5 0.1 reshape.87
  53.6 39.9 %psum.15 = f32[2,64]{1,0:T(2,128)S(1)} all-reduce(f32[2,64]{1,0:T(2,128)S(1)} %reshape.87), channel_id=1, replica_groups=mesh['group'=1,'ctx'=32] {'ctx'}, use_global_device_ids=true, to_apply=%region_4.0 | all-reduce | flops 128 | bytes 1024 | tf_op jit(solution)/shard_map/psum | solution.py:57
  93.5 0.1 broadcast_bitcast_fusion
  93.6 0.2 reduce_window_sum.11
  93.8 0.1 copy.37
  93.9 0.1 add.113
  94.0 77.3 %all-reduce.2.cloned.1.call-done = f32[2,8192]{1,0:T(2,128)} async-done(((f32[2,8192]{1,0:T(2,128)}), f32[2,8192]{1,0:T(2,128)}) %all-reduce.2.cloned.1.call-update) | async-done | bytes 65552 | tf_op jit(solution)/shard_map/psum | solution.py:57
  171.3 0.0 copy-done
  171.3 1.1 fusion.32
  172.3 1.7 collective-permute-start
  174.1 0.1 compare_select_fusion
  174.1 0.8 collective-permute-done
  174.9 1.5 collective-permute-start.1
  176.5 2.4 %collective-permute-done.1 = f32[2,4096]{1,0:T(2,128)S(1)} collective-permute-done((f32[2,4096]{1,0:T(2,128)S(1)}, f32[2,4096]{1,0:T(2,128)S(1)}, u32[]{:S(2)}, u32[]{:S(2)}) %collective-permute-start.1) | collective-permute-done | bytes 32800 | tf_op jit(solution)/shard_map/ppermute | solution.py:67
  178.9 1.5 collective-permute-start.2
  180.5 2.4 %collective-permute-done.2 = f32[2,4096]{1,0:T(2,128)S(1)} collective-permute-done((f32[2,4096]{1,0:T(2,128)S(1)}, f32[2,4096]{1,0:T(2,128)S(1)}, u32[]{:S(2)}, u32[]{:S(2)}) %collective-permute-start.2) | collective-permute-done | bytes 32800 | tf_op jit(solution)/shard_map/ppermute | solution.py:67
  182.9 1.6 collective-permute-start.3
  184.5 0.2 convolution_convert_fusion.1
  184.7 0.0 copy-done.3
  184.7 0.1 reshape.100
  184.8 2.1 collective-permute-done.3
  186.9 1.9 collective-permute-start.4
  188.8 0.1 convolution_bitcast_fusion
  188.9 0.1 reshape.93
  189.0 2.8 %collective-permute-done.4 = f32[2,4096]{1,0:T(2,128)S(1)} collective-permute-done((f32[2,4096]{1,0:T(2,128)S(1)}, f32[2,4096]{1,0:T(2,128)S(1)}, u32[]{:S(2)}, u32[]{:S(2)}) %collective-permute-start.4) | collective-permute-done | bytes 32800 | tf_op jit(solution)/shard_map/ppermute | solution.py:67
  191.8 0.0 copy-done.1
  191.8 0.1 multiply_reduce_fusion
  192.0 0.0 copy-done.2
  192.0 0.2 convolution_convert_fusion
  192.2 1.9 fusion.4
  194.1 3.7 %fusion.6 = bf16[2,32,128]{2,0,1:T(2,128)(2,1)} fusion(bf16[1,192,4096]{2,1,0:T(8,128)(2,1)} %param.19, bf16[2,4096]{1,0:T(2,128)(2,1)S(1)} %convolution_convert_fusion, bf16[1,4096,192]{1,2,0:T(8,128)(2,1)} %param.18, f32[2]{0:T(128)S(1)} %convolution_bitcast_fusion, f32[2,192]{1,0:T(2,128)S(1)} %fusion.4), kind=kOutput, calls=%fused_computation.10 | convolution fusion | flops 6310144 | bytes 3180040 | tf_op jit(solution)/shard_map/dot_general | solution.py:97
  197.8 4.5 %all-to-all-start = ((bf16[2,32,128]{2,0,1:T(2,128)(2,1)}), bf16[2,32,128]{2,0,1:T(2,128)(2,1)S(1)}, u32[]{:S(2)}, u32[]{:S(2)}) async-start(bf16[2,32,128]{2,0,1:T(2,128)(2,1)} %fusion.6), calls=%async_computation | async-start | bytes 32768 | tf_op jit(solution)/shard_map/all_to_all | solution.py:99
  202.3 7.2 %all-to-all-done = bf16[2,32,128]{2,0,1:T(2,128)(2,1)S(1)} async-done(((bf16[2,32,128]{2,0,1:T(2,128)(2,1)}), bf16[2,32,128]{2,0,1:T(2,128)(2,1)S(1)}, u32[]{:S(2)}, u32[]{:S(2)}) %all-to-all-start) | async-done | bytes 16416 | tf_op jit(solution)/shard_map/all_to_all | solution.py:99
  209.5 0.6 gather_fusion
  210.1 0.6 dynamic-slice_add_fusion
  (12 shorter events, 0.2 us)
Async XLA Ops:
  6.5 164.7 %copy-start = (bf16[256,4096]{1,0:T(8,128)(2,1)S(1)}, bf16[256,4096]{1,0:T(8,128)(2,1)}, u32[]{:S(2)}) copy-start(bf16[256,4096]{1,0:T(8,128)(2,1)} %param.14) | copy-start | bytes 6291460
  6.5 164.7 %all-reduce.2.cloned.1.call-start = ((), (), s32[]{:S(2)}) async-start(), calls=%async_computation.1 | async-start | bytes 131072 | tf_op jit(solution)/shard_map/psum | solution.py:57
  51.2 133.6 %copy-start.3 = (f32[2,4]{1,0:T(2,128)S(1)}, f32[2,4]{1,0:T(2,128)}, u32[]{:S(2)}) copy-start(f32[2,4]{1,0:T(2,128)} %param.21) | copy-start | bytes 100
  51.2 140.7 %copy-start.1 = (bf16[2,4096]{1,0:T(2,128)(2,1)S(1)}, bf16[2,4096]{1,0:T(2,128)(2,1)}, u32[]{:S(2)}) copy-start(bf16[2,4096]{1,0:T(2,128)(2,1)} %param.15) | copy-start | bytes 49156
  51.8 140.1 %copy-start.2 = (f32[4096]{0:T(1024)S(1)}, f32[4096]{0:T(1024)}, u32[]{:S(2)}) copy-start(f32[4096]{0:T(1024)} %param.16) | copy-start | bytes 49156
  172.3 2.6 %collective-permute-start = (f32[2,4096]{1,0:T(2,128)S(1)}, f32[2,4096]{1,0:T(2,128)S(1)}, u32[]{:S(2)}, u32[]{:S(2)}) collective-permute-start(f32[2,4096]{1,0:T(2,128)S(1)} %fusion.32), channel_id=1, source_target_pairs={{0,1},{1,0},{2,3},{3,2},{4,5},{5,4},{6,7},{7,6},{8,9},{9,8},{10,11... | collective-permute-start | bytes 98312 | tf_op jit(solution)/shard_map/ppermute | solution.py:67
  174.9 4.0 %collective-permute-start.1 = (f32[2,4096]{1,0:T(2,128)S(1)}, f32[2,4096]{1,0:T(2,128)S(1)}, u32[]{:S(2)}, u32[]{:S(2)}) collective-permute-start(f32[2,4096]{1,0:T(2,128)S(1)} %add.101), channel_id=1, source_target_pairs={{0,2},{1,3},{2,0},{3,1},{4,6},{5,7},{6,4},{7,5},{8,10},{9,11},{10,... | collective-permute-start | bytes 98312 | tf_op jit(solution)/shard_map/ppermute | solution.py:67
  178.9 4.0 %collective-permute-start.2 = (f32[2,4096]{1,0:T(2,128)S(1)}, f32[2,4096]{1,0:T(2,128)S(1)}, u32[]{:S(2)}, u32[]{:S(2)}) collective-permute-start(f32[2,4096]{1,0:T(2,128)S(1)} %add.102), channel_id=1, source_target_pairs={{0,4},{1,5},{2,6},{3,7},{4,0},{5,1},{6,2},{7,3},{8,12},{9,13},{10,... | collective-permute-start | bytes 98312 | tf_op jit(solution)/shard_map/ppermute | solution.py:67
  182.9 4.0 %collective-permute-start.3 = (f32[2,4096]{1,0:T(2,128)S(1)}, f32[2,4096]{1,0:T(2,128)S(1)}, u32[]{:S(2)}, u32[]{:S(2)}) collective-permute-start(f32[2,4096]{1,0:T(2,128)S(1)} %add.103), channel_id=1, source_target_pairs={{0,8},{1,9},{2,10},{3,11},{4,12},{5,13},{6,14},{7,15},{8,0},{9,1},... | collective-permute-start | bytes 98312 | tf_op jit(solution)/shard_map/ppermute | solution.py:67
  186.9 4.9 %collective-permute-start.4 = (f32[2,4096]{1,0:T(2,128)S(1)}, f32[2,4096]{1,0:T(2,128)S(1)}, u32[]{:S(2)}, u32[]{:S(2)}) collective-permute-start(f32[2,4096]{1,0:T(2,128)S(1)} %add.104), channel_id=1, source_target_pairs={{0,16},{1,17},{2,18},{3,19},{4,20},{5,21},{6,22},{7,23},{8,24},{9,... | collective-permute-start | bytes 98312 | tf_op jit(solution)/shard_map/ppermute | solution.py:67
  197.8 11.7 %all-to-all-start = ((bf16[2,32,128]{2,0,1:T(2,128)(2,1)}), bf16[2,32,128]{2,0,1:T(2,128)(2,1)S(1)}, u32[]{:S(2)}, u32[]{:S(2)}) async-start(bf16[2,32,128]{2,0,1:T(2,128)(2,1)} %fusion.6), calls=%async_computation | async-start | bytes 32768 | tf_op jit(solution)/shard_map/all_to_all | solution.py:99
Sparse Core Ops, SparseCore 0:
  52.0 119.2 all-reduce.1
